TPU v7x, 32 devices: a whole 2x2x4 slice. The times are simulated.
32 devices in a mesh: dp: 4 (over x, core), ctx: 8 (over z, y).
Axes of the slice: x: 2, y: 2, z: 4, core: 2. Of those that a mesh axis runs over, the one named last changes fastest.
Arguments:
- tokens: bfloat16 [4096, 1792], P(('dp', 'ctx')), may hold values from -6 to 6
- cotangent: bfloat16 [4096, 1792], P(('dp', 'ctx')), may hold values from -6 to 6
- expert_ids: int32 [4096, 4], P(('dp', 'ctx')), may hold values from 0 to 15, all different within a row; in each aligned block of 128 rows (0 to 127, 128 to 255, ...) at most 40 rows name the same one
- norm_gain: float32 [1792], replicated, may hold values from 0.5 to 1.5
- router_weight: bfloat16 [1792, 16], replicated, may hold values from -0.125 to 0.125
- gate_weight: bfloat16 [16, 1792, 1536], P('ctx', None, 'dp'), may hold values from -0.125 to 0.125
- up_weight: bfloat16 [16, 1792, 1536], P('ctx', None, 'dp'), may hold values from -0.125 to 0.125
- down_weight: bfloat16 [16, 1536, 1792], P('ctx', 'dp'), may hold values from -0.15625 to 0.15625
Outputs:
- grad_tokens: bfloat16 [4096, 1792], P(('dp', 'ctx'))
- grad_gate: bfloat16 [16, 1792, 1536], P('ctx', None, 'dp')
- grad_up: bfloat16 [16, 1792, 1536], P('ctx', None, 'dp')
- grad_down: bfloat16 [16, 1536, 1792], P('ctx', 'dp')
- grad_router: float32 [1792, 16], P(('dp', 'ctx'))
- grad_gain: float32 [1792], P(('dp', 'ctx'))
Inputs may be any that keep to these rules, and one draw needn't show every extreme that they name: `expert_ids`: each row names 4 different experts; among the rows of one device no expert is named more than 40 times.
All inputs are finite; a program needn't handle non-finite values.
Results may differ from a plain program's by a relative error of at most 0.02.
Values may be sent and summed in bfloat16 or wider, within the bound.
No kernel may reach another device: no remote copies, remote signals or barrier semaphores. Data moves between devices by JAX's collectives and lax.ppermute only.
A program may use at most 192 MiB of HBM per device.

v0:
```python
import jax
import jax.numpy as jnp
from jax import lax
from jax.sharding import PartitionSpec as P

EPSILON = 1e-05
SWISH_SCALE = 1.702


def expert_pass(rows, upstream, weight, gate_weight, up_weight, down_weight):
    gate_pre = jnp.einsum("prd,pdf->prf", rows, gate_weight, preferred_element_type=jnp.float32)
    up_pre = jnp.einsum("prd,pdf->prf", rows, up_weight, preferred_element_type=jnp.float32)
    squash = jax.nn.sigmoid(SWISH_SCALE * gate_pre)
    hidden = (gate_pre * squash * (up_pre + 1.0)).astype(jnp.bfloat16)
    grad_out = jnp.einsum("prd,pfd->prf", upstream, down_weight, preferred_element_type=jnp.float32)
    score = jnp.sum(grad_out * hidden.astype(jnp.float32), axis=2)
    grad_hidden = weight[:, :, None] * grad_out
    slope = squash + SWISH_SCALE * gate_pre * squash * (1.0 - squash)
    grad_pre_gate = (grad_hidden * (up_pre + 1.0) * slope).astype(jnp.bfloat16)
    grad_pre_up = (grad_hidden * gate_pre * squash).astype(jnp.bfloat16)
    scaled_up = (weight[:, :, None] * upstream.astype(jnp.float32)).astype(jnp.bfloat16)
    down_grad = jnp.einsum(
        "prf,prd->pfd", hidden, scaled_up, preferred_element_type=jnp.float32
    ).astype(jnp.bfloat16)
    gate_grad = jnp.einsum(
        "prd,prf->pdf", rows, grad_pre_gate, preferred_element_type=jnp.float32
    ).astype(jnp.bfloat16)
    up_grad = jnp.einsum(
        "prd,prf->pdf", rows, grad_pre_up, preferred_element_type=jnp.float32
    ).astype(jnp.bfloat16)
    back = jnp.einsum(
        "prf,pdf->prd", grad_pre_gate, gate_weight, preferred_element_type=jnp.float32
    )
    back = back + jnp.einsum(
        "prf,pdf->prd", grad_pre_up, up_weight, preferred_element_type=jnp.float32
    )
    return (gate_grad, up_grad, down_grad, back, score)


def body(
    tokens, cotangent, expert_ids, norm_gain, router_weight, gate_weight, up_weight, down_weight
):
    ctx_size = lax.axis_size("ctx")
    local = gate_weight.shape[0]
    experts = router_weight.shape[1]
    rows_here = tokens.shape[0]
    picks = expert_ids.shape[1]
    width = tokens.shape[1]
    assigned = rows_here * picks
    capacity = max(2, rows_here * picks * 5 // (4 * experts))
    slots = experts * capacity
    widened = tokens.astype(jnp.float32)
    inverse = lax.rsqrt(jnp.mean(widened * widened, axis=1, keepdims=True) + EPSILON)
    scaled = widened * inverse
    normed = (scaled * norm_gain).astype(jnp.bfloat16)
    logits = jnp.dot(normed, router_weight, preferred_element_type=jnp.float32)
    labels = jnp.arange(experts, dtype=jnp.int32)
    member = expert_ids[:, :, None] == labels
    chosen = jnp.sum(jnp.where(member, logits[:, None, :], 0.0), axis=2)
    lifted = jnp.exp(chosen)
    gates = lifted / jnp.sum(lifted, axis=1, keepdims=True)
    hits = member.reshape(assigned, experts).astype(jnp.int32)
    rank = jnp.sum((jnp.cumsum(hits, axis=0) - 1) * hits, axis=1)
    position = expert_ids.reshape(-1) * capacity + rank
    match = (jnp.arange(slots, dtype=jnp.int32)[:, None] == position[None, :]).astype(jnp.float32)
    dispatch = jnp.sum(match.reshape(slots, rows_here, picks), axis=2)
    dispatch_low = dispatch.astype(jnp.bfloat16)
    out_rows = jnp.dot(dispatch_low, normed, preferred_element_type=jnp.float32).astype(
        jnp.bfloat16
    )
    out_rows = out_rows.reshape(ctx_size, local, capacity, width)
    out_grad = jnp.dot(dispatch_low, cotangent, preferred_element_type=jnp.float32).astype(
        jnp.bfloat16
    )
    out_grad = out_grad.reshape(ctx_size, local, capacity, width)
    out_gate = jnp.dot(match, gates.reshape(-1), precision=lax.Precision.HIGHEST)
    out_gate = out_gate.reshape(ctx_size, local, capacity)
    arrived = (
        lax.all_to_all(out_rows, "ctx", split_axis=0, concat_axis=2, tiled=True),
        lax.all_to_all(out_grad, "ctx", split_axis=0, concat_axis=2, tiled=True),
        lax.all_to_all(
            out_gate.astype(jnp.bfloat16), "ctx", split_axis=0, concat_axis=2, tiled=True
        ).astype(out_gate.dtype),
    )
    rows, upstream, weight = (
        lax.all_gather(arrived[0], "dp", axis=2, tiled=True),
        lax.all_gather(arrived[1], "dp", axis=2, tiled=True),
        lax.all_gather(arrived[2].astype(jnp.bfloat16), "dp", axis=2, tiled=True).astype(
            jnp.float32
        ),
    )
    gate_grad, up_grad, down_grad, back, score = expert_pass(
        rows[0], upstream[0], weight[0], gate_weight, up_weight, down_weight
    )
    back_mine, score_mine = (
        lax.psum_scatter(back.astype(jnp.bfloat16), "dp", scatter_dimension=1, tiled=True).astype(
            jnp.float32
        ),
        lax.psum_scatter(score.astype(jnp.bfloat16), "dp", scatter_dimension=1, tiled=True).astype(
            jnp.float32
        ),
    )
    back_slots, score_slots = (
        lax.all_to_all(
            back_mine.astype(jnp.bfloat16), "ctx", split_axis=1, concat_axis=0, tiled=True
        ).astype(back_mine.dtype),
        lax.all_to_all(
            score_mine.astype(jnp.bfloat16), "ctx", split_axis=1, concat_axis=0, tiled=True
        ).astype(score_mine.dtype),
    )
    back_flat = back_slots.reshape(slots, width)
    score_flat = score_slots.reshape(slots)
    grad_tok = jnp.dot(dispatch.T, back_flat, precision=lax.Precision.HIGHEST)
    score_tok = jnp.dot(score_flat, match, precision=lax.Precision.HIGHEST).reshape(
        rows_here, picks
    )
    mixed = jnp.sum(gates * score_tok, axis=1, keepdims=True)
    grad_chosen = gates * (score_tok - mixed)
    grad_logits = jnp.sum(jnp.where(member, grad_chosen[:, :, None], 0.0), axis=1).astype(
        jnp.bfloat16
    )
    grad_normed = grad_tok + jnp.dot(
        grad_logits, router_weight.T, preferred_element_type=jnp.float32
    )
    router_part = jnp.dot(normed.T, grad_logits, preferred_element_type=jnp.float32)
    gain_part = jnp.sum(grad_normed * scaled, axis=0)
    router_grad, gain_grad = (
        lax.psum_scatter(router_part, ("dp", "ctx"), scatter_dimension=0, tiled=True),
        lax.psum_scatter(gain_part, ("dp", "ctx"), scatter_dimension=0, tiled=True),
    )
    grad_scaled = grad_normed * norm_gain
    correction = jnp.mean(grad_scaled * scaled, axis=1, keepdims=True)
    grad_input = (
        cotangent.astype(jnp.float32) + inverse * (grad_scaled - scaled * correction)
    ).astype(jnp.bfloat16)
    return (grad_input, gate_grad, up_grad, down_grad, router_grad, gain_grad)


def solution(mesh):
    return jax.shard_map(
        body,
        mesh=mesh,
        in_specs=(
            P(("dp", "ctx"), None),
            P(("dp", "ctx"), None),
            P(("dp", "ctx"), None),
            P(),
            P(),
            P("ctx", None, "dp"),
            P("ctx", None, "dp"),
            P("ctx", "dp", None),
        ),
        out_specs=(
            P(("dp", "ctx"), None),
            P("ctx", None, "dp"),
            P("ctx", None, "dp"),
            P("ctx", "dp", None),
            P(("dp", "ctx"), None),
            P(("dp", "ctx")),
        ),
        check_vma=False,
    )
```

profile of v0, /device:TPU:0, one launch (start us, length us, event | category | flops | bytes accessed | tf_op | source)
XLA Modules:
  0.0 604.0 jit_solution(15963162471281344825)
XLA Ops:
  14.0 59.6 %all_to_all.85 = bf16[8,2,40,1792]{3,2,1,0:T(8,128)(2,1)S(1)} all-to-all(bf16[8,2,40,1792]{3,2,1,0:T(8,128)(2,1)S(1)} %bitcast.98), channel_id=1, replica_groups=mesh['dp'=4,'ctx'=8] {'ctx'}, dimensions={0} | all-to-all | bytes 4587520 | tf_op jit(solution)/shard_map/all_to_all | solution.py:79
  76.0 55.6 %all_to_all.86 = bf16[8,2,40,1792]{3,2,1,0:T(8,128)(2,1)S(1)} all-to-all(bf16[8,2,40,1792]{3,2,1,0:T(8,128)(2,1)S(1)} %bitcast.99), channel_id=1, replica_groups=mesh['dp'=4,'ctx'=8] {'ctx'}, dimensions={0} | all-to-all | bytes 4587520 | tf_op jit(solution)/shard_map/all_to_all | solution.py:80
  137.8 9.5 %fusion.5 = f32[2,1280,384]{1,2,0:T(8,128)} fusion(bf16[2,1792,384]{2,1,0:T(8,128)(2,1)S(1)} %copy-done, bf16[1,2,1280,1792]{3,2,1,0:T(8,128)(2,1)} %all-gather.5.cloned.1.call-done), kind=kOutput, calls=%fused_computation.7 | convolution fusion | flops 3523215360 | bytes 15859712 | tf_op jit(solution)/shard_map/prd,pdf->prf/dot_general | solution.py:11
  147.3 11.2 %fusion.13 = f32[2,1280,384]{1,2,0:T(8,128)} fusion(bf16[2,1792,384]{2,1,0:T(8,128)(2,1)S(1)} %copy-done.6, bf16[1,2,1280,1792]{3,2,1,0:T(8,128)(2,1)} %all-gather.5.cloned.1.call-done), kind=kOutput, calls=%fused_computation.15 | convolution fusion | flops 3524198400 | bytes 15859712 | tf_op jit(solution)/shard_map/prd,pdf->prf/dot_general | solution.py:12
  158.5 43.5 %all-gather.3.cloned.1.call-done = bf16[1,2,1280,1792]{3,2,1,0:T(8,128)(2,1)} async-done(((bf16[1,2,320,1792]{3,2,1,0:T(8,128)(2,1)}), bf16[1,2,1280,1792]{3,2,1,0:T(8,128)(2,1)}) %all-gather.3.cloned.1.call-update) | async-done | bytes 9175056 | tf_op jit(solution)/shard_map/all_gather | solution.py:87
  201.9 13.7 %multiply_reduce_fusion = (bf16[2,1280]{1,0:T(2,128)(2,1)}, bf16[2,1280,384]{1,2,0:T(8,128)(2,1)}, f32[2,1280,384]{1,2,0:T(8,128)}) fusion(f32[2,1280,384]{1,2,0:T(8,128)} %fusion.13, f32[2,1280,384]{1,2,0:T(8,128)} %fusion.5, bf16[2,384,1792]{2,1,0:T(8,128)(2,1)} %param.15, bf16[1,2,1280,1792]{3,2,1,0:T(8,128)(2,1)} %all-gather.3.cloned.1.call-done), kind=kOutput, calls=%fused_computation.16 | convolution fusion | flops 3533043200 | bytes 25695232 | tf_op jit(solution)/shard_map/prd,pfd->prf/dot_general | solution.py:15
  217.9 20.0 %reduce-scatter.8.cloned.1.call-done = bf16[320,2]{1,0:T(8,128)(2,1)} async-done(((bf16[1280,2]{1,0:T(8,128)(2,1)}), bf16[320,2]{1,0:T(8,128)(2,1)}) %reduce-scatter.8.cloned.1.call-update) | async-done | bytes 1296
  239.5 5.5 all-to-all-start.4
  245.8 2.1 eq.110
  247.9 3.6 all-to-all-done.4
  262.0 8.9 %all_to_all.87 = bf16[8,2,40]{2,1,0:T(2,128)(2,1)S(1)} all-to-all(bf16[8,2,40]{2,1,0:T(2,128)(2,1)S(1)} %convert_element_type.83), channel_id=1, replica_groups=mesh['dp'=4,'ctx'=8] {'ctx'}, dimensions={0} | all-to-all | bytes 2560 | tf_op jit(solution)/shard_map/all_to_all | solution.py:81
  274.4 7.1 %all_gather.9 = bf16[1,2,1280]{1,0,2:T(2,128)(2,1)S(1)} all-gather(bf16[1,2,320]{1,0,2:T(2,128)(2,1)} %copy.141), channel_id=1, replica_groups=mesh['dp'=4,'ctx'=8] {'dp'}, dimensions={2}, use_global_device_ids=true | all-gather | bytes 6400 | tf_op jit(solution)/shard_map/all_gather | solution.py:88
  284.8 6.4 %multiply_convert_fusion.3 = (bf16[2,1280,384]{1,2,0:T(8,128)(2,1)}, bf16[2,1280,384]{1,2,0:T(8,128)(2,1)S(1)}) fusion(f32[2,1280,384]{1,2,0:T(8,128)} %fusion.5, f32[2,1280,384]{1,2,0:T(8,128)} %get-tuple-element.14, f32[2,1280]{1,0:T(2,128)} %copy.142, f32[2,1280,384]{1,2,0:T(8,128)} %fusion.13), kind=kLoop, calls=%fused_computation.18 | loop fusion | flops 14745600 | bytes 15738880 | tf_op jit(solution)/shard_map/convert_element_type | solution.py:20
  291.3 9.3 %fusion.52 = f32[2,1280,1792]{2,1,0:T(8,128)} fusion(bf16[2,1280,384]{1,2,0:T(8,128)(2,1)S(1)} %get-tuple-element.13, bf16[2,1792,384]{2,1,0:T(8,128)(2,1)S(1)} %copy-done), kind=kOutput, calls=%fused_computation.77 | convolution fusion | flops 3523215360 | bytes 23068672 | tf_op jit(solution)/shard_map/prf,pdf->prd/dot_general | solution.py:31
  300.6 16.4 %add_convert_fusion = bf16[2,1280,1792]{2,1,0:T(8,128)(2,1)} fusion(f32[2,1280,1792]{2,1,0:T(8,128)} %fusion.52, bf16[2,1280,384]{1,2,0:T(8,128)(2,1)} %get-tuple-element.12, bf16[2,1792,384]{2,1,0:T(8,128)(2,1)} %param.14), kind=kOutput, calls=%fused_computation.1 | convolution fusion | flops 3532390400 | bytes 32243712 | tf_op jit(solution)/shard_map/prf,pdf->prd/dot_general | solution.py:34
  317.1 73.6 %reduce-scatter.6.cloned.1.call-done = bf16[2,320,1792]{2,1,0:T(8,128)(2,1)} async-done(((bf16[2,1280,1792]{2,1,0:T(8,128)(2,1)}), bf16[2,320,1792]{2,1,0:T(8,128)(2,1)}) %reduce-scatter.6.cloned.1.call-update) | async-done | bytes 2293776 | tf_op jit(solution)/shard_map/reduce_scatter | solution.py:96
  390.7 5.4 copy.149
  396.1 5.5 all-to-all-start.3
  403.0 12.0 %fusion.20 = bf16[2,1792,384]{2,1,0:T(8,128)(2,1)} fusion(bf16[2,1280,384]{1,2,0:T(8,128)(2,1)} %get-tuple-element.12, bf16[1,2,1280,1792]{3,2,1,0:T(8,128)(2,1)} %all-gather.5.cloned.1.call-done), kind=kOutput, calls=%fused_computation.23 | convolution fusion | flops 3524591616 | bytes 13893632 | tf_op jit(solution)/shard_map/prd,prf->pdf/dot_general | solution.py:28
  415.0 9.7 %fusion.16 = bf16[2,384,1792]{2,1,0:T(8,128)(2,1)} fusion(bf16[2,1280,384]{1,2,0:T(8,128)(2,1)} %get-tuple-element.11, bf16[1,2,1280,1792]{3,2,1,0:T(8,128)(2,1)} %all-gather.3.cloned.1.call-done, f32[2,1280]{1,0:T(2,128)S(1)} %copy-done.10), kind=kOutput, calls=%fused_computation.21 | convolution fusion | flops 3538354176 | bytes 13903872 | tf_op jit(solution)/shard_map/prf,prd->pfd/dot_general | solution.py:22
  424.7 12.3 %fusion.17 = bf16[2,1792,384]{2,1,0:T(8,128)(2,1)} fusion(bf16[2,1280,384]{1,2,0:T(8,128)(2,1)S(1)} %copy-done.3, bf16[1,2,1280,1792]{3,2,1,0:T(8,128)(2,1)} %all-gather.5.cloned.1.call-done), kind=kOutput, calls=%fused_computation.22 | convolution fusion | flops 3524591616 | bytes 13893632 | tf_op jit(solution)/shard_map/prd,prf->pdf/dot_general | solution.py:25
  437.0 111.5 %all-reduce.4.cloned.1.call-done = f32[1792,16]{0,1:T(8,128)} async-done(((f32[1792,16]{0,1:T(8,128)}), f32[1792,16]{0,1:T(8,128)}) %all-reduce.4.cloned.1.call-update) | async-done | bytes 114704
  553.0 41.1 %all-reduce.1 = f32[1792]{0:T(1024)S(1)} all-reduce(f32[1792]{0:T(1024)S(1)} %get-tuple-element.6), channel_id=5, replica_groups=mesh['dp'=4,'ctx'=8] {'dp','ctx'}, use_global_device_ids=true, to_apply=%region_15.16.clone | all-reduce | flops 1792 | bytes 14336
  594.7 2.5 fusion.34
  (103 shorter events, 43.5 us)
Async XLA Ops:
  7.2 130.6 %copy-start = (bf16[2,1792,384]{2,1,0:T(8,128)(2,1)S(1)}, bf16[2,1792,384]{2,1,0:T(8,128)(2,1)}, u32[]{:S(2)}) copy-start(bf16[2,1792,384]{2,1,0:T(8,128)(2,1)} %param.13) | copy-start | bytes 8257540
  7.2 130.6 %all-gather.5.cloned.1.call-start = ((), (), s32[]{:S(2)}) async-start(), calls=%async_computation.8 | async-start | bytes 11468800 | tf_op jit(solution)/shard_map/all_gather | solution.py:86
  9.6 64.1 %copy-start.16 = (f32[128]{0:T(128)}, f32[128]{0:T(128)S(1)}, u32[]{:S(2)}) copy-start(f32[128]{0:T(128)S(1)} %add_rsqrt_fusion) | copy-start | bytes 1540
  11.1 2.9 copy-start.12
  73.7 1.6 copy-start.7
  75.2 126.7 %all-gather.3.cloned.1.call-start = ((), (), s32[]{:S(2)}) async-start(), calls=%async_computation.7 | async-start | bytes 11468800 | tf_op jit(solution)/shard_map/all_gather | solution.py:87
  131.6 2.1 copy-start.4
  131.6 2.1 copy-start.8
  131.7 3.3 copy-start.11
  133.2 104.7 %reduce-scatter.8.cloned.1.call-start = ((), (), s32[]{:S(2)}) async-start(), calls=%async_computation.10 | async-start | bytes 409600
  137.8 9.5 %copy-start.6 = (bf16[2,1792,384]{2,1,0:T(8,128)(2,1)S(1)}, bf16[2,1792,384]{2,1,0:T(8,128)(2,1)}, u32[]{:S(2)}) copy-start(bf16[2,1792,384]{2,1,0:T(8,128)(2,1)} %param.14) | copy-start | bytes 8257540
  158.5 86.8 %copy-start.14 = (f32[128,4]{0,1:T(4,128)S(1)}, f32[128,4]{0,1:T(4,128)}, u32[]{:S(2)}) copy-start(f32[128,4]{0,1:T(4,128)} %select_reduce_fusion.2) | copy-start | bytes 6148
  239.5 12.0 %all-to-all-start.4 = ((bf16[2,8,40]{2,0,1:T(2,128)(2,1)}), bf16[2,8,40]{2,0,1:T(2,128)(2,1)}, u32[]{:S(2)}, u32[]{:S(2)}) async-start(bf16[2,8,40]{2,0,1:T(2,128)(2,1)} %copy.152), calls=%async_computation.5 | async-start | bytes 8192 | tf_op jit(solution)/shard_map/all_to_all | solution.py:107
  245.0 145.7 %reduce-scatter.6.cloned.1.call-start = ((), (), s32[]{:S(2)}) async-start(), calls=%async_computation.9 | async-start | bytes 11468800 | tf_op jit(solution)/shard_map/reduce_scatter | solution.py:96
  291.3 9.4 %copy-start.2 = (bf16[2,1280,384]{1,2,0:T(8,128)(2,1)}, bf16[2,1280,384]{1,2,0:T(8,128)(2,1)S(1)}, u32[]{:S(2)}) copy-start(bf16[2,1280,384]{1,2,0:T(8,128)(2,1)S(1)} %get-tuple-element.13) | copy-start | bytes 5898244
  317.0 84.9 %copy-start.13 = (f32[128,4]{0,1:T(4,128)S(1)}, f32[128,4]{0,1:T(4,128)}, u32[]{:S(2)}) copy-start(f32[128,4]{0,1:T(4,128)} %get-tuple-element.9) | copy-start | bytes 6148
  317.1 84.9 %copy-start.19 = (f32[128]{0:T(128)S(1)}, f32[128]{0:T(128)}, u32[]{:S(2)}) copy-start(f32[128]{0:T(128)} %get-tuple-element.8) | copy-start | bytes 1540
  317.1 84.9 %copy-start.17 = (f32[128]{0:T(128)S(1)}, f32[128]{0:T(128)}, u32[]{:S(2)}) copy-start(f32[128]{0:T(128)} %copy-done.16) | copy-start | bytes 1540
  396.1 153.7 %all-to-all-start.3 = ((bf16[2,320,1792]{2,0,1:T(2,128)(2,1)}), bf16[2,320,1792]{2,0,1:T(2,128)(2,1)S(1)}, u32[]{:S(2)}, u32[]{:S(2)}) async-start(bf16[2,320,1792]{2,0,1:T(2,128)(2,1)} %copy.149), calls=%async_computation.4 | async-start | bytes 4587520 | tf_op jit(solution)/shard_map/all_to_all | solution.py:104
  401.6 146.8 %all-reduce.4.cloned.1.call-start = ((), (), s32[]{:S(2)}) async-start(), calls=%async_computation.11 | async-start | bytes 229376
  403.0 12.0 %copy-start.10 = (f32[2,1280]{1,0:T(2,128)S(1)}, f32[2,1280]{1,0:T(2,128)}, u32[]{:S(2)}) copy-start(f32[2,1280]{1,0:T(2,128)} %copy.142) | copy-start | bytes 30724
  415.0 9.7 %copy-start.3 = (bf16[2,1280,384]{1,2,0:T(8,128)(2,1)S(1)}, bf16[2,1280,384]{1,2,0:T(8,128)(2,1)}, u32[]{:S(2)}) copy-start(bf16[2,1280,384]{1,2,0:T(8,128)(2,1)} %copy-done.2) | copy-start | bytes 5898244
  550.0 1.6 copy-start.5
  550.2 46.9 %copy-start.1 = (bf16[2,1792,384]{2,1,0:T(8,128)(2,1)S(1)}, bf16[2,1792,384]{2,1,0:T(8,128)(2,1)}, u32[]{:S(2)}) copy-start(bf16[2,1792,384]{2,1,0:T(8,128)(2,1)} %param.13) | copy-start | bytes 8257540
  (3 other events, 3.7 us)
Sparse Core Ops, SparseCore 0:
  75.3 61.6 all-gather.4
  139.2 62.7 all-gather.2
  217.4 20.4 reduce-scatter.7
  317.2 73.4 reduce-scatter.5
  408.3 140.1 all-reduce.3
where the time goes:
time: 608 us; the launch traced here: 604 us
  waiting for transfers between devices  252 us (41%)
  blocking collectives  172 us (28%)
  matrix products  103 us (17%)
  local copies, waits for them, and re-layouts  28.2 us (5%)
  other arithmetic  21.1 us (3%)
  between operations  14.4 us (2%)
  starting transfers between devices  12.2 us (2%)
    unnamed x7, waiting for transfers between devices  132 us
    reduce_scatter x1, waiting for transfers between devices, body(): lax.psum_scatter(back.astype(jnp.bfloat16), 'dp', scatter_dimension=1, ti...  73.6 us
    all_to_all x1, blocking collectives, body(): lax.all_to_all(out_rows, 'ctx', split_axis=0, concat_axis=2, tiled=True)  59.6 us
    all_to_all x1, blocking collectives, body(): lax.all_to_all(out_grad, 'ctx', split_axis=0, concat_axis=2, tiled=True)  55.6 us
    all_gather x1, waiting for transfers between devices, body(): lax.all_gather(arrived[1], 'dp', axis=2, tiled=True)  43.5 us
    unnamed x1, blocking collectives  41.1 us
    dot_general x1, matrix products, expert_pass(): jnp.einsum('prf,pdf->prd', grad_pre_up, up_weight, preferred_element_type...  16.4 us
    dot_general x1, matrix products, expert_pass(): jnp.einsum('prd,pfd->prf', upstream, down_weight, preferred_element_type=...  13.7 us
  transfers between devices with their start and end apart: 7, of which 5 were waited for; matrix products, arithmetic and copies ran while one was open for 11% of the time, Pallas kernels for 0%

commit v1 on v0

--- a/solution.py
+++ b/solution.py
@@ -5,6 +5,12 @@
 
 EPSILON = 1e-05
 SWISH_SCALE = 1.702
+
+
+def swap_blocks(x, name, split, join):
+    pieces = jnp.split(x, lax.axis_size(name), axis=split)
+    arrived = lax.all_to_all(jnp.stack(pieces), name, 0, 0)
+    return jnp.concatenate(arrived, axis=join)
 
 
 def expert_pass(rows, upstream, weight, gate_weight, up_weight, down_weight):
@@ -77,7 +83,7 @@
     out_gate = out_gate.reshape(ctx_size, local, capacity)
     arrived = (
         lax.all_to_all(out_rows, "ctx", split_axis=0, concat_axis=2, tiled=True),
-        lax.all_to_all(out_grad, "ctx", split_axis=0, concat_axis=2, tiled=True),
+        swap_blocks(out_grad, "ctx", 0, 2),
         lax.all_to_all(
             out_gate.astype(jnp.bfloat16), "ctx", split_axis=0, concat_axis=2, tiled=True
         ).astype(out_gate.dtype),

time: 608 us -> 609 us (level)
  no operation moved by 1% of the time
where the time goes in v1:
time: 609 us; the launch traced here: 604 us
  waiting for transfers between devices  252 us (41%)
  blocking collectives  172 us (28%)
  matrix products  103 us (17%)
  local copies, waits for them, and re-layouts  28.9 us (5%)
  other arithmetic  21.1 us (3%)
  between operations  14.4 us (2%)
  starting transfers between devices  12.3 us (2%)
    unnamed x7, waiting for transfers between devices  132 us
    reduce_scatter x1, waiting for transfers between devices, body(): lax.psum_scatter(back.astype(jnp.bfloat16), 'dp', scatter_dimension=1, ti...  73.7 us
    all_to_all x1, blocking collectives, body(): lax.all_to_all(out_rows, 'ctx', split_axis=0, concat_axis=2, tiled=True)  59.6 us
    all_to_all x1, blocking collectives, swap_blocks(): arrived = lax.all_to_all(jnp.stack(pieces), name, 0, 0)  55.6 us
    all_gather x1, waiting for transfers between devices, body(): lax.all_gather(arrived[1], 'dp', axis=2, tiled=True)  43 us
    unnamed x1, blocking collectives  41.1 us
    dot_general x1, matrix products, expert_pass(): jnp.einsum('prf,pdf->prd', grad_pre_up, up_weight, preferred_element_type...  16.4 us
    dot_general x1, matrix products, expert_pass(): jnp.einsum('prd,pfd->prf', upstream, down_weight, preferred_element_type=...  13.7 us
  transfers between devices with their start and end apart: 7, of which 5 were waited for; matrix products, arithmetic and copies ran while one was open for 11% of the time, Pallas kernels for 0%

profile of v1, /device:TPU:0, one launch (start us, length us, event | category | flops | bytes accessed | tf_op | source)
XLA Modules:
  0.0 604.5 jit_solution(15081805893570523623)
XLA Ops:
  14.4 59.6 %all_to_all.72 = bf16[8,2,40,1792]{3,2,1,0:T(8,128)(2,1)S(1)} all-to-all(bf16[8,2,40,1792]{3,2,1,0:T(8,128)(2,1)S(1)} %bitcast.103), channel_id=1, replica_groups=mesh['dp'=4,'ctx'=8] {'ctx'}, dimensions={0} | all-to-all | bytes 4587520 | tf_op jit(solution)/shard_map/all_to_all | solution.py:85
  76.8 55.6 %all_to_all.73 = bf16[8,1,2,40,1792]{4,3,2,1,0:T(8,128)(2,1)S(1)} all-to-all(bf16[8,1,2,40,1792]{4,3,2,1,0:T(8,128)(2,1)S(1)} %constant_dynamic-update-slice_fusion), channel_id=1, replica_groups=mesh['dp'=4,'ctx'=8] {'ctx'}, dimensions={0} | all-to-all | bytes 4587520 | tf_op jit(solution)/shard_map/all_to_all | solution.py:12
  138.6 9.6 %fusion.5 = f32[2,1280,384]{1,2,0:T(8,128)} fusion(bf16[2,1792,384]{2,1,0:T(8,128)(2,1)S(1)} %copy-done, bf16[1,2,1280,1792]{3,2,1,0:T(8,128)(2,1)} %all-gather.5.cloned.1.call-done), kind=kOutput, calls=%fused_computation.7 | convolution fusion | flops 3523215360 | bytes 15859712 | tf_op jit(solution)/shard_map/prd,pdf->prf/dot_general | solution.py:17
  148.1 11.2 %fusion.13 = f32[2,1280,384]{1,2,0:T(8,128)} fusion(bf16[2,1792,384]{2,1,0:T(8,128)(2,1)S(1)} %copy-done.6, bf16[1,2,1280,1792]{3,2,1,0:T(8,128)(2,1)} %all-gather.5.cloned.1.call-done), kind=kOutput, calls=%fused_computation.15 | convolution fusion | flops 3524198400 | bytes 15859712 | tf_op jit(solution)/shard_map/prd,pdf->prf/dot_general | solution.py:18
  159.3 43.0 %all-gather.3.cloned.1.call-done = bf16[1,2,1280,1792]{3,2,1,0:T(8,128)(2,1)} async-done(((bf16[1,2,320,1792]{3,2,1,0:T(8,128)(2,1)}), bf16[1,2,1280,1792]{3,2,1,0:T(8,128)(2,1)}) %all-gather.3.cloned.1.call-update) | async-done | bytes 9175056 | tf_op jit(solution)/shard_map/all_gather | solution.py:93
  202.3 13.7 %multiply_reduce_fusion = (bf16[2,1280]{1,0:T(2,128)(2,1)}, bf16[2,1280,384]{1,2,0:T(8,128)(2,1)}, f32[2,1280,384]{1,2,0:T(8,128)}) fusion(f32[2,1280,384]{1,2,0:T(8,128)} %fusion.13, f32[2,1280,384]{1,2,0:T(8,128)} %fusion.5, bf16[2,384,1792]{2,1,0:T(8,128)(2,1)} %param.15, bf16[1,2,1280,1792]{3,2,1,0:T(8,128)(2,1)} %all-gather.3.cloned.1.call-done), kind=kOutput, calls=%fused_computation.16 | convolution fusion | flops 3533043200 | bytes 25695232 | tf_op jit(solution)/shard_map/prd,pfd->prf/dot_general | solution.py:21
  218.3 20.0 %reduce-scatter.8.cloned.1.call-done = bf16[320,2]{1,0:T(8,128)(2,1)} async-done(((bf16[1280,2]{1,0:T(8,128)(2,1)}), bf16[320,2]{1,0:T(8,128)(2,1)}) %reduce-scatter.8.cloned.1.call-update) | async-done | bytes 1296
  239.9 5.5 all-to-all-start.4
  246.2 2.1 eq.110
  248.3 3.6 all-to-all-done.4
  262.4 8.9 %all_to_all.74 = bf16[8,2,40]{2,1,0:T(2,128)(2,1)S(1)} all-to-all(bf16[8,2,40]{2,1,0:T(2,128)(2,1)S(1)} %convert_element_type.83), channel_id=1, replica_groups=mesh['dp'=4,'ctx'=8] {'ctx'}, dimensions={0} | all-to-all | bytes 2560 | tf_op jit(solution)/shard_map/all_to_all | solution.py:87
  274.7 7.1 %all_gather.9 = bf16[1,2,1280]{1,0,2:T(2,128)(2,1)S(1)} all-gather(bf16[1,2,320]{1,0,2:T(2,128)(2,1)} %copy.141), channel_id=1, replica_groups=mesh['dp'=4,'ctx'=8] {'dp'}, dimensions={2}, use_global_device_ids=true | all-gather | bytes 6400 | tf_op jit(solution)/shard_map/all_gather | solution.py:94
  285.2 6.4 %multiply_convert_fusion.3 = (bf16[2,1280,384]{1,2,0:T(8,128)(2,1)}, bf16[2,1280,384]{1,2,0:T(8,128)(2,1)S(1)}) fusion(f32[2,1280,384]{1,2,0:T(8,128)} %fusion.5, f32[2,1280,384]{1,2,0:T(8,128)} %get-tuple-element.22, f32[2,1280]{1,0:T(2,128)} %copy.142, f32[2,1280,384]{1,2,0:T(8,128)} %fusion.13), kind=kLoop, calls=%fused_computation.18 | loop fusion | flops 14745600 | bytes 15738880 | tf_op jit(solution)/shard_map/convert_element_type | solution.py:26
  291.6 9.3 %fusion.53 = f32[2,1280,1792]{2,1,0:T(8,128)} fusion(bf16[2,1280,384]{1,2,0:T(8,128)(2,1)S(1)} %get-tuple-element.13, bf16[2,1792,384]{2,1,0:T(8,128)(2,1)S(1)} %copy-done), kind=kOutput, calls=%fused_computation.86 | convolution fusion | flops 3523215360 | bytes 23068672 | tf_op jit(solution)/shard_map/prf,pdf->prd/dot_general | solution.py:37
  301.0 16.4 %add_convert_fusion = bf16[2,1280,1792]{2,1,0:T(8,128)(2,1)} fusion(f32[2,1280,1792]{2,1,0:T(8,128)} %fusion.53, bf16[2,1280,384]{1,2,0:T(8,128)(2,1)} %get-tuple-element.12, bf16[2,1792,384]{2,1,0:T(8,128)(2,1)} %param.14), kind=kOutput, calls=%fused_computation.1 | convolution fusion | flops 3532390400 | bytes 32243712 | tf_op jit(solution)/shard_map/prf,pdf->prd/dot_general | solution.py:40
  317.4 73.7 %reduce-scatter.6.cloned.1.call-done = bf16[2,320,1792]{2,1,0:T(8,128)(2,1)} async-done(((bf16[2,1280,1792]{2,1,0:T(8,128)(2,1)}), bf16[2,320,1792]{2,1,0:T(8,128)(2,1)}) %reduce-scatter.6.cloned.1.call-update) | async-done | bytes 2293776 | tf_op jit(solution)/shard_map/reduce_scatter | solution.py:102
  391.1 5.4 copy.149
  396.5 5.7 all-to-all-start.3
  403.5 12.0 %fusion.20 = bf16[2,1792,384]{2,1,0:T(8,128)(2,1)} fusion(bf16[2,1280,384]{1,2,0:T(8,128)(2,1)} %get-tuple-element.12, bf16[1,2,1280,1792]{3,2,1,0:T(8,128)(2,1)} %all-gather.5.cloned.1.call-done), kind=kOutput, calls=%fused_computation.23 | convolution fusion | flops 3524591616 | bytes 13893632 | tf_op jit(solution)/shard_map/prd,prf->pdf/dot_general | solution.py:34
  415.5 9.7 %fusion.16 = bf16[2,384,1792]{2,1,0:T(8,128)(2,1)} fusion(bf16[2,1280,384]{1,2,0:T(8,128)(2,1)} %get-tuple-element.11, bf16[1,2,1280,1792]{3,2,1,0:T(8,128)(2,1)} %all-gather.3.cloned.1.call-done, f32[2,1280]{1,0:T(2,128)S(1)} %copy-done.10), kind=kOutput, calls=%fused_computation.21 | convolution fusion | flops 3538354176 | bytes 13903872 | tf_op jit(solution)/shard_map/prf,prd->pfd/dot_general | solution.py:28
  425.2 12.3 %fusion.17 = bf16[2,1792,384]{2,1,0:T(8,128)(2,1)} fusion(bf16[2,1280,384]{1,2,0:T(8,128)(2,1)S(1)} %copy-done.3, bf16[1,2,1280,1792]{3,2,1,0:T(8,128)(2,1)} %all-gather.5.cloned.1.call-done), kind=kOutput, calls=%fused_computation.22 | convolution fusion | flops 3524591616 | bytes 13893632 | tf_op jit(solution)/shard_map/prd,prf->pdf/dot_general | solution.py:31
  437.5 111.5 %all-reduce.4.cloned.1.call-done = f32[1792,16]{0,1:T(8,128)} async-done(((f32[1792,16]{0,1:T(8,128)}), f32[1792,16]{0,1:T(8,128)}) %all-reduce.4.cloned.1.call-update) | async-done | bytes 114704
  553.5 41.1 %all-reduce.1 = f32[1792]{0:T(1024)S(1)} all-reduce(f32[1792]{0:T(1024)S(1)} %get-tuple-element.6), channel_id=5, replica_groups=mesh['dp'=4,'ctx'=8] {'dp','ctx'}, use_global_device_ids=true, to_apply=%region_15.16.clone | all-reduce | flops 1792 | bytes 14336
  595.2 2.5 fusion.34
  (112 shorter events, 44.2 us)
Async XLA Ops:
  7.2 131.4 %copy-start = (bf16[2,1792,384]{2,1,0:T(8,128)(2,1)S(1)}, bf16[2,1792,384]{2,1,0:T(8,128)(2,1)}, u32[]{:S(2)}) copy-start(bf16[2,1792,384]{2,1,0:T(8,128)(2,1)} %param.13) | copy-start | bytes 8257540
  7.2 131.4 %all-gather.5.cloned.1.call-start = ((), (), s32[]{:S(2)}) async-start(), calls=%async_computation.8 | async-start | bytes 11468800 | tf_op jit(solution)/shard_map/all_gather | solution.py:92
  9.6 64.4 %copy-start.16 = (f32[128]{0:T(128)}, f32[128]{0:T(128)S(1)}, u32[]{:S(2)}) copy-start(f32[128]{0:T(128)S(1)} %add_rsqrt_fusion) | copy-start | bytes 1540
  74.0 1.6 copy-start.7
  75.6 126.7 %all-gather.3.cloned.1.call-start = ((), (), s32[]{:S(2)}) async-start(), calls=%async_computation.7 | async-start | bytes 11468800 | tf_op jit(solution)/shard_map/all_gather | solution.py:93
  132.4 2.1 copy-start.4
  132.4 2.1 copy-start.8
  132.4 3.3 copy-start.11
  134.0 104.3 %reduce-scatter.8.cloned.1.call-start = ((), (), s32[]{:S(2)}) async-start(), calls=%async_computation.10 | async-start | bytes 409600
  138.5 9.6 %copy-start.6 = (bf16[2,1792,384]{2,1,0:T(8,128)(2,1)S(1)}, bf16[2,1792,384]{2,1,0:T(8,128)(2,1)}, u32[]{:S(2)}) copy-start(bf16[2,1792,384]{2,1,0:T(8,128)(2,1)} %param.14) | copy-start | bytes 8257540
  159.3 86.3 %copy-start.14 = (f32[128,4]{0,1:T(4,128)S(1)}, f32[128,4]{0,1:T(4,128)}, u32[]{:S(2)}) copy-start(f32[128,4]{0,1:T(4,128)} %select_reduce_fusion.2) | copy-start | bytes 6148
  239.9 12.0 %all-to-all-start.4 = ((bf16[2,8,40]{2,0,1:T(2,128)(2,1)}), bf16[2,8,40]{2,0,1:T(2,128)(2,1)}, u32[]{:S(2)}, u32[]{:S(2)}) async-start(bf16[2,8,40]{2,0,1:T(2,128)(2,1)} %copy.152), calls=%async_computation.5 | async-start | bytes 8192 | tf_op jit(solution)/shard_map/all_to_all | solution.py:113
  245.4 145.7 %reduce-scatter.6.cloned.1.call-start = ((), (), s32[]{:S(2)}) async-start(), calls=%async_computation.9 | async-start | bytes 11468800 | tf_op jit(solution)/shard_map/reduce_scatter | solution.py:102
  291.6 9.4 %copy-start.2 = (bf16[2,1280,384]{1,2,0:T(8,128)(2,1)}, bf16[2,1280,384]{1,2,0:T(8,128)(2,1)S(1)}, u32[]{:S(2)}) copy-start(bf16[2,1280,384]{1,2,0:T(8,128)(2,1)S(1)} %get-tuple-element.13) | copy-start | bytes 5898244
  396.5 6.0 copy-start.13
  396.5 6.0 copy-start.19
  396.5 6.0 copy-start.17
  396.5 153.9 %all-to-all-start.3 = ((bf16[2,320,1792]{2,0,1:T(2,128)(2,1)}), bf16[2,320,1792]{2,0,1:T(2,128)(2,1)S(1)}, u32[]{:S(2)}, u32[]{:S(2)}) async-start(bf16[2,320,1792]{2,0,1:T(2,128)(2,1)} %copy.149), calls=%async_computation.4 | async-start | bytes 4587520 | tf_op jit(solution)/shard_map/all_to_all | solution.py:110
  402.1 146.8 %all-reduce.4.cloned.1.call-start = ((), (), s32[]{:S(2)}) async-start(), calls=%async_computation.11 | async-start | bytes 229376
  403.5 12.0 %copy-start.10 = (f32[2,1280]{1,0:T(2,128)S(1)}, f32[2,1280]{1,0:T(2,128)}, u32[]{:S(2)}) copy-start(f32[2,1280]{1,0:T(2,128)} %copy.142) | copy-start | bytes 30724
  415.5 9.7 %copy-start.3 = (bf16[2,1280,384]{1,2,0:T(8,128)(2,1)S(1)}, bf16[2,1280,384]{1,2,0:T(8,128)(2,1)}, u32[]{:S(2)}) copy-start(bf16[2,1280,384]{1,2,0:T(8,128)(2,1)} %copy-done.2) | copy-start | bytes 5898244
  550.7 1.4 copy-start.5
  550.7 1.4 copy-start.9
  550.7 46.9 %copy-start.1 = (bf16[2,1792,384]{2,1,0:T(8,128)(2,1)S(1)}, bf16[2,1792,384]{2,1,0:T(8,128)(2,1)}, u32[]{:S(2)}) copy-start(bf16[2,1792,384]{2,1,0:T(8,128)(2,1)} %param.13) | copy-start | bytes 8257540
  (3 other events, 2.5 us)
Sparse Core Ops, SparseCore 0:
  75.7 61.6 all-gather.4
  139.5 62.7 all-gather.2
  217.8 20.4 reduce-scatter.7
  317.5 73.4 reduce-scatter.5
  408.8 140.1 all-reduce.3
